TPU v7x, 128 devices: a whole 4x4x4 slice. The times are simulated.
128 devices in a mesh: seq: 16 (over z, x), exp: 8 (over y, core).
Axes of the slice: x: 4, y: 4, z: 4, core: 2. Of those that a mesh axis runs over, the one named last changes fastest.
Arguments:
- tokens: bfloat16 [8, 2048, 4096], P('exp', 'seq'), may hold values from -6 to 6
- out_grad: bfloat16 [8, 2048, 4096], P('exp', 'seq'), may hold values from -0.59765625 to 0.59765625
- router_weight: bfloat16 [4096, 128], replicated, may hold values from -8 to 8
- gate_weight: bfloat16 [128, 4096, 768], P(('seq', 'exp')), may hold values from -0.09375 to 0.09375
- up_weight: bfloat16 [128, 4096, 768], P(('seq', 'exp')), may hold values from -0.09375 to 0.09375
- down_weight: bfloat16 [128, 768, 4096], P(('seq', 'exp')), may hold values from -0.21875 to 0.21875
- saved_gate: bfloat16 [128, 2048, 768], P(('seq', 'exp')), may hold values from -6 to 6
- saved_up: bfloat16 [128, 2048, 768], P(('seq', 'exp')), may hold values from -6 to 6
- expert_ids: int32 [8, 2048, 8], P('exp', 'seq'), may hold values from 0 to 127, as said below
- aux_weight: float32 [1], replicated, may hold values from 2 to 6
Outputs:
- token_grad: bfloat16 [8, 2048, 4096], P('exp', 'seq')
- combine_grad: float32 [8, 2048, 8], P('exp', 'seq')
- router_grad: float32 [4096, 128], P(('seq', 'exp'))
Inputs may be any that keep to these rules, and one draw needn't show every extreme that they name: `expert_ids`: among the rows of one device (128 tokens) each expert is named at most 16 times, and some expert exactly 16 times; a token's 8 experts differ.
All inputs are finite; a program needn't handle non-finite values.
Results may differ from a plain program's by a relative error of at most 0.013.
Values may be sent and summed in bfloat16 or wider, within the bound.
A program may use at most 192 MiB of HBM per device.

v0:
```python
import functools
import jax
import jax.numpy as jnp
from jax import lax
from jax.sharding import Mesh
from jax.sharding import PartitionSpec as P

SEQ = ("seq_0", "seq_1")
EXP = ("exp_0", "exp_1")
SEQ_EXP = ("seq_0", "seq_1", "exp_0", "exp_1")


def over_axes(shard, axes):
    return functools.reduce(lax.psum, axes, shard)


def in_blocks(shard, dim, size):
    shape = shard.shape
    parts = shard.reshape(*shape[:dim], size, shape[dim] // size, *shape[dim + 1 :])
    return jnp.moveaxis(parts, dim, 0)


def summed_on_arrival(shard, axis, dim):
    size = lax.axis_size(axis)
    parts = lax.all_to_all(in_blocks(shard, dim, size), axis, 0, 0, tiled=True)
    return jnp.sum(parts, axis=0)


def summed_rows(shard, axes, dim):
    far, near = axes
    own = summed_on_arrival(in_blocks(shard, dim, lax.axis_size(far)), near, dim + 1)
    return jnp.sum(lax.all_to_all(own, far, 0, 0, tiled=True), axis=0)


def filled_up(lines, size):
    spare = -len(lines) % size
    return jnp.pad(lines, [(0, spare)] + [(0, 0)] * (lines.ndim - 1))


def from_everyone(shard, axis):
    size = lax.axis_size(axis)
    return lax.all_to_all(
        jnp.broadcast_to(shard[None], (size, *shard.shape)), axis, 0, 0, tiled=True
    )


def laid_out(parts, dim):
    shape = list(parts.shape[1:])
    shape[dim] *= parts.shape[0]
    return jnp.moveaxis(parts, 0, dim).reshape(shape)


def gathered_by_axis(shard, axes, dim):
    far, near = axes
    parts = from_everyone(from_everyone(shard, far), near)
    return laid_out(parts.swapaxes(0, 1).reshape(-1, *shard.shape), dim)


def total_of(shard, axes):
    lines = shard.reshape(-1, shard.shape[-1])
    own = summed_rows(filled_up(lines, lax.axis_size(axes[0]) * lax.axis_size(axes[1])), axes, 0)
    whole = gathered_by_axis(own, axes, 0)
    return whole[: len(lines)].reshape(shard.shape)


def expert_backward(grad_rows, gate_rows, w_gate, w_up, w_down, pre_gate, pre_up):
    upstream = jnp.einsum("rd,fd->rf", grad_rows, w_down, preferred_element_type=jnp.float32)
    first = pre_gate.astype(jnp.float32)
    second = pre_up.astype(jnp.float32)
    gate_sig = jax.nn.sigmoid(first)
    gate_act = first * gate_sig
    hidden = gate_act * second
    slot_combine = jnp.sum(upstream * hidden, axis=-1).astype(jnp.bfloat16)
    scaled = gate_rows.astype(jnp.float32)[:, None] * upstream
    grad_first = (scaled * second * gate_sig * (1.0 + first * (1.0 - gate_sig))).astype(
        jnp.bfloat16
    )
    grad_second = (scaled * gate_act).astype(jnp.bfloat16)
    back_rows = jnp.einsum("rf,df->rd", grad_first, w_gate, preferred_element_type=jnp.float32)
    back_rows = back_rows + jnp.einsum(
        "rf,df->rd", grad_second, w_up, preferred_element_type=jnp.float32
    )
    return (back_rows.astype(jnp.bfloat16), slot_combine)


def shards(
    tokens,
    out_grad,
    router_weight,
    gate_weight,
    up_weight,
    down_weight,
    saved_gate,
    saved_up,
    expert_ids,
    aux_weight,
):
    seq_size = lax.axis_size(SEQ)
    exp_size = lax.axis_size(EXP)
    devices = seq_size * exp_size
    inputs = tokens[0]
    upstream_grad = out_grad[0]
    chosen_ids = expert_ids[0]
    tok_rows, top_count = chosen_ids.shape
    model_width = inputs.shape[1]
    experts = router_weight.shape[1]
    capacity = saved_gate.shape[1] // devices
    logits = jnp.dot(inputs, router_weight, preferred_element_type=jnp.float32)
    router_probs = jax.nn.softmax(logits, axis=-1)
    chosen = jnp.take_along_axis(router_probs, chosen_ids, axis=1)
    chosen_sum = jnp.sum(chosen, axis=1, keepdims=True)
    gate_vals = chosen / chosen_sum
    onehot = (
        chosen_ids.reshape(-1)[:, None] == jnp.arange(experts, dtype=jnp.int32)[None, :]
    ).astype(jnp.int32)
    rank_before = jnp.cumsum(onehot, axis=0) - onehot
    slot_pos = jnp.sum(rank_before * onehot, axis=1)
    slot_index = chosen_ids.reshape(-1) * capacity + slot_pos
    token_order = jnp.arange(tok_rows * top_count, dtype=jnp.int32) // top_count
    slot_token = (
        jnp.full((experts * capacity,), tok_rows, jnp.int32).at[slot_index].set(token_order)
    )
    grad_padded = jnp.concatenate(
        [upstream_grad, jnp.zeros((1, model_width), jnp.bfloat16)], axis=0
    )
    grad_slots = grad_padded[slot_token]
    gate_slots = (
        jnp.zeros((experts * capacity,), jnp.bfloat16)
        .at[slot_index]
        .set(gate_vals.reshape(-1).astype(jnp.bfloat16))
    )
    chosen_count = jnp.sum(onehot.reshape(tok_rows, top_count, experts), axis=1).astype(jnp.float32)
    local_counts = jnp.sum(chosen_count, axis=0)
    seq_counts = over_axes(local_counts, SEQ)
    recv_grad, recv_gate = (
        lax.all_to_all(
            grad_slots.reshape(experts, 1, capacity, model_width),
            SEQ_EXP,
            split_axis=0,
            concat_axis=1,
            tiled=True,
        ),
        lax.all_to_all(
            gate_slots.reshape(experts, 1, capacity),
            SEQ_EXP,
            split_axis=0,
            concat_axis=1,
            tiled=True,
        ),
    )
    back_rows, slot_combine = expert_backward(
        recv_grad.reshape(-1, model_width),
        recv_gate.reshape(-1),
        gate_weight[0],
        up_weight[0],
        down_weight[0],
        saved_gate[0],
        saved_up[0],
    )
    returned, combine_back = (
        lax.all_to_all(
            back_rows.reshape(1, devices, capacity, model_width),
            SEQ_EXP,
            split_axis=1,
            concat_axis=0,
            tiled=True,
        ),
        lax.all_to_all(
            slot_combine.reshape(1, devices, capacity),
            SEQ_EXP,
            split_axis=1,
            concat_axis=0,
            tiled=True,
        ),
    )
    returned_rows = returned.reshape(experts * capacity, model_width)
    expert_sum = jnp.sum(
        returned_rows[slot_index].reshape(tok_rows, top_count, model_width).astype(jnp.float32),
        axis=1,
    )
    combine_grad = (
        combine_back.reshape(-1)[slot_index].reshape(tok_rows, top_count).astype(jnp.float32)
    )
    prob_sel = (
        combine_grad - jnp.sum(gate_vals * combine_grad, axis=1, keepdims=True)
    ) / chosen_sum
    prob_grad = jnp.einsum(
        "tk,tke->te", prob_sel, onehot.reshape(tok_rows, top_count, experts).astype(jnp.float32)
    )
    fraction = experts * seq_counts / (top_count * tok_rows * seq_size)
    prob_grad = prob_grad + aux_weight[0] * fraction[None, :]
    dlogits = router_probs * (prob_grad - jnp.sum(router_probs * prob_grad, axis=1, keepdims=True))
    logit_grad = dlogits.astype(jnp.bfloat16)
    token_grad = expert_sum + jnp.einsum(
        "te,de->td", logit_grad, router_weight, preferred_element_type=jnp.float32
    )
    own_rows = model_width // devices
    router_full = total_of(
        jnp.einsum("td,te->de", inputs, logit_grad, preferred_element_type=jnp.float32),
        (("seq_0", "seq_1", "exp_0"), "exp_1"),
    )
    router_grad = lax.dynamic_slice_in_dim(
        router_full, lax.axis_index(SEQ_EXP) * own_rows, own_rows, 0
    )
    return (token_grad.astype(jnp.bfloat16)[None], combine_grad[None], router_grad)


def solution(mesh):
    torus = Mesh(mesh.devices.reshape(4, 4, 4, 2), ("seq_0", "seq_1", "exp_0", "exp_1"))
    return jax.shard_map(
        shards,
        mesh=torus,
        in_specs=(
            P(EXP, SEQ, None),
            P(EXP, SEQ, None),
            P(),
            P(SEQ_EXP, None, None),
            P(SEQ_EXP, None, None),
            P(SEQ_EXP, None, None),
            P(SEQ_EXP, None, None),
            P(SEQ_EXP, None, None),
            P(EXP, SEQ, None),
            P(),
        ),
        out_specs=(P(EXP, SEQ, None), P(EXP, SEQ, None), P(SEQ_EXP, None)),
        check_vma=False,
    )
```

profile of v0, /device:TPU:82, one launch (start us, length us, event | category | flops | bytes accessed | tf_op | source)
XLA Modules:
  0.0 671.6 jit_solution(18006657790768191358)
XLA Ops:
  0.6 0.9 copy.61
  1.5 0.1 eq.36
  1.6 0.1 eq.32
  1.7 0.7 broadcast_multiply_fusion
  2.4 0.1 copy.63
  2.5 0.2 fusion.28
  2.8 0.1 copy.64
  2.9 0.1 copy.60
  3.0 0.1 mul.87
  3.1 0.4 fusion.27
  3.5 4.3 scatter_custom_fusion.1
  7.8 1.3 concatenate.3
  9.2 14.3 %gather_fusion = bf16[2048,4096]{1,0:T(8,128)(2,1)} fusion(bf16[129,4096]{1,0:T(8,128)(2,1)S(1)} %concatenate.3, s32[2048]{0:T(1024)S(1)} %fusion.34), kind=kCustom, calls=%fused_computation | custom fusion | bytes 33562624 | tf_op jit(solution)/shard_map/gather | solution.py:126
  23.5 10.4 %all-to-all-start.1 = ((bf16[128,1,16,4096]{3,2,1,0:T(8,128)(2,1)}), bf16[128,1,16,4096]{3,2,1,0:T(8,128)(2,1)}, u32[]{:S(2)}, u32[]{:S(2)}) async-start(bf16[128,1,16,4096]{3,2,1,0:T(8,128)(2,1)} %bitcast.94), calls=%async_computation.1 | async-start | bytes 33554432 | tf_op jit(solution)/shard_map/all_to_all | solution.py:136
  33.9 4.8 copy.70
  38.7 4.7 copy.69
  43.4 0.1 copy.65
  43.5 0.1 reshape.225
  43.7 0.6 fusion.48
  44.3 7.0 %gather_fusion.3 = f32[1024]{0:T(1024)S(1)} fusion(f32[128,128]{0,1:T(8,128)S(1)} %fusion.32, s32[1024]{0:T(1024)S(1)} %reshape.225), kind=kCustom, calls=%fused_computation.3 | custom fusion | bytes 16384 | tf_op jit(solution)/shard_map/jit(take_along_axis)/gather | solution.py:110
  52.1 0.1 fusion.35
  52.2 0.1 div.43
  52.4 7.6 %scatter_custom_fusion = bf16[2048]{0:T(1024)(128)(2,1)S(1)} fusion(s32[1024]{0:T(1024)S(1)} %bitcast.104, bf16[1024]{0:T(1024)(128)(2,1)S(1)} %divide_convert_fusion, bf16[]{:T(256)} %constant.29.clone.1), kind=kCustom, calls=%fused_computation.88 | custom fusion | bytes 4098 | tf_op jit(solution)/shard_map/scatter | solution.py:130
  60.0 0.7 reshape.251
  60.7 0.2 convert_reduce_fusion.1
  61.0 116.0 %psum.14 = f32[128]{0:T(128)S(1)} all-reduce(f32[128]{0:T(128)S(1)} %convert_reduce_fusion.3), channel_id=1, replica_groups=mesh['seq_0'=4,'seq_1'=4,'exp_0'=4,'exp_1'=2] {'seq_0'}, use_global_device_ids=true, to_apply=%region_13.14 | all-reduce | flops 128 | bytes 1024 | tf_op jit(solution)/shard_map/psum | solution.py:14
  177.0 62.2 %psum.15 = f32[128]{0:T(128)S(1)} all-reduce(f32[128]{0:T(128)S(1)} %psum.14), channel_id=1, replica_groups=mesh['seq_0'=4,'seq_1'=4,'exp_0'=4,'exp_1'=2] {'seq_1'}, use_global_device_ids=true, to_apply=%region_14.15 | all-reduce | flops 128 | bytes 1024 | tf_op jit(solution)/shard_map/psum | solution.py:14
  239.2 8.9 %all-to-all-done.1 = bf16[128,1,16,4096]{3,2,1,0:T(8,128)(2,1)} async-done(((bf16[128,1,16,4096]{3,2,1,0:T(8,128)(2,1)}), bf16[128,1,16,4096]{3,2,1,0:T(8,128)(2,1)}, u32[]{:S(2)}, u32[]{:S(2)}) %all-to-all-start.1) | async-done | bytes 16777248 | tf_op jit(solution)/shard_map/all_to_all | solution.py:136
  248.0 15.1 %all-to-all-start = ((bf16[128,1,16]{2,1,0:T(2,128)(2,1)}), bf16[128,1,16]{2,1,0:T(2,128)(2,1)S(1)}, u32[]{:S(2)}, u32[]{:S(2)}) async-start(bf16[128,1,16]{2,1,0:T(2,128)(2,1)} %reshape.251), calls=%async_computation | async-start | bytes 131072 | tf_op jit(solution)/shard_map/all_to_all | solution.py:143
  263.1 22.5 %fusion.4 = (bf16[2048]{0:T(1024)(128)(2,1)S(1)}, f32[2048,768]{0,1:T(8,128)}) fusion(bf16[1,2048,768]{1,2,0:T(8,128)(2,1)} %copy.69, bf16[1,2048,768]{1,2,0:T(8,128)(2,1)} %copy.70, bf16[2048,4096]{1,0:T(8,128)(2,1)} %bitcast.11, bf16[1,768,4096]{2,1,0:T(8,128)(2,1)} %param.15), kind=kOutput, calls=%fused_computation.17 | convolution fusion | flops 12899055616 | bytes 35655680 | tf_op jit(solution)/shard_map/rd,fd->rf/dot_general | solution.py:67
  285.7 0.7 convert_element_type.124
  286.4 9.8 %all-to-all-start.3 = ((bf16[1,128,16]{2,0,1:T(2,128)(2,1)}), bf16[1,128,16]{2,0,1:T(2,128)(2,1)S(1)}, u32[]{:S(2)}, u32[]{:S(2)}) async-start(bf16[1,128,16]{2,0,1:T(2,128)(2,1)} %convert_element_type.124), calls=%async_computation.3 | async-start | bytes 131072 | tf_op jit(solution)/shard_map/all_to_all | solution.py:168
  296.2 0.2 convert_reduce_fusion.2
  296.5 4.9 all-to-all-done.3
  301.3 0.2 reduce.1
  301.5 0.1 reshape.194
  301.6 6.8 %gather_fusion.2 = bf16[1024]{0:T(1024)(128)(2,1)S(1)} fusion(bf16[2048]{0:T(1024)(128)(2,1)S(1)} %reshape.194, s32[1024]{0:T(1024)S(1)} %broadcast_clamp_fusion), kind=kCustom, calls=%fused_computation.2 | custom fusion | bytes 8192 | tf_op jit(solution)/shard_map/gather | solution.py:182
  308.5 0.2 multiply_reduce_fusion.1
  308.7 0.1 subtract_divide_fusion
  308.8 0.3 fusion.25
  309.2 0.1 copy.78
  309.3 0.1 multiply_reduce_fusion
  309.4 0.1 multiply_convert_fusion.2
  309.5 1.8 convolution_bitcast_fusion
  311.3 1.9 copy.73
  313.2 0.2 copy.74
  313.4 5.4 all_to_all.56
  318.8 1.2 reduce_sum.111
  320.0 9.7 %all-to-all-start.5 = ((f32[64,32,128]{2,1,0:T(8,128)}), f32[64,32,128]{2,1,0:T(8,128)S(1)}, u32[]{:S(2)}, u32[]{:S(2)}) async-start(f32[64,32,128]{2,1,0:T(8,128)} %reduce_sum.111), calls=%async_computation.5 | async-start | bytes 2097152 | tf_op jit(solution)/shard_map/all_to_all | solution.py:32
  329.7 29.5 %fusion.10 = f32[2048,4096]{1,0:T(8,128)} fusion(bf16[1,4096,768]{2,1,0:T(8,128)(2,1)} %param.13, f32[2048,768]{0,1:T(8,128)} %get-tuple-element.18, bf16[1,2048,768]{1,2,0:T(8,128)(2,1)} %copy.69, bf16[1,2048,768]{1,2,0:T(8,128)(2,1)} %copy.70, f32[2048]{0:T(1024)S(1)} %reshape.195), kind=kOutput, calls=%fused_computation.23 | convolution fusion | flops 12905349120 | bytes 52436992 | tf_op jit(solution)/shard_map/rf,df->rd/dot_general | solution.py:79
  359.3 0.1 reduce_sum.112
  359.4 1.1 broadcast_in_dim.24
  360.5 10.3 %all-to-all-start.6 = ((f32[64,32,128]{2,1,0:T(8,128)}), f32[64,32,128]{2,1,0:T(8,128)S(1)}, u32[]{:S(2)}, u32[]{:S(2)}) async-start(f32[64,32,128]{2,1,0:T(8,128)} %broadcast_in_dim.24), calls=%async_computation.6 | async-start | bytes 2097152 | tf_op jit(solution)/shard_map/all_to_all | solution.py:42
  370.8 27.9 %add_convert_fusion = bf16[2048,4096]{1,0:T(8,128)(2,1)} fusion(f32[2048,4096]{1,0:T(8,128)} %fusion.10, bf16[1,4096,768]{2,1,0:T(8,128)(2,1)} %param.14, f32[2048,768]{0,1:T(8,128)} %get-tuple-element.18, f32[2048]{0:T(1024)S(1)} %reshape.195, bf16[1,2048,768]{1,2,0:T(8,128)(2,1)} %copy.70), kind=kOutput, calls=%fused_computation.6 | convolution fusion | flops 12914262016 | bytes 66068480 | tf_op jit(solution)/shard_map/rf,df->rd/dot_general | solution.py:80
  398.7 0.2 broadcast_in_dim.25
  399.0 5.4 all_to_all.57
  404.4 10.6 %all-to-all-start.2 = ((bf16[1,128,16,4096]{3,2,0,1:T(8,128)(2,1)}), bf16[1,128,16,4096]{3,2,0,1:T(8,128)(2,1)}, u32[]{:S(2)}, u32[]{:S(2)}) async-start(bf16[1,128,16,4096]{3,2,0,1:T(8,128)(2,1)} %bitcast.95), calls=%async_computation.2 | async-start | bytes 33554432 | tf_op jit(solution)/shard_map/all_to_all | solution.py:161
  415.1 0.7 copy.76
  415.8 0.2 copy.75
  416.0 0.6 constant_dynamic-slice_fusion
  416.6 219.9 %all-to-all-done.2 = bf16[1,128,16,4096]{3,2,0,1:T(8,128)(2,1)} async-done(((bf16[1,128,16,4096]{3,2,0,1:T(8,128)(2,1)}), bf16[1,128,16,4096]{3,2,0,1:T(8,128)(2,1)}, u32[]{:S(2)}, u32[]{:S(2)}) %all-to-all-start.2) | async-done | bytes 16777248 | tf_op jit(solution)/shard_map/all_to_all | solution.py:161
  636.5 23.1 %gather_fusion.1 = bf16[1024,4096]{1,0:T(8,128)(2,1)} fusion(bf16[2048,4096]{1,0:T(8,128)(2,1)} %bitcast.20, s32[1024]{0:T(1024)S(1)} %broadcast_clamp_fusion), kind=kCustom, calls=%fused_computation.1 | custom fusion | bytes 16781312 | tf_op jit(solution)/shard_map/gather | solution.py:178
  659.6 9.1 %convert_reduce_fusion = f32[128,4096]{1,0:T(8,128)S(1)} fusion(bf16[1024,4096]{1,0:T(8,128)(2,1)} %gather_fusion.1), kind=kLoop, calls=%fused_computation.7 | loop fusion | flops 7864320 | bytes 10485760 | tf_op jit(solution)/shard_map/reduce_sum | solution.py:177
  668.7 2.7 fusion.15
  (30 shorter events, 0.7 us)
Async XLA Ops:
  0.6 43.0 %copy-start = (bf16[1,128,4096]{2,1,0:T(8,128)(2,1)S(1)}, bf16[1,128,4096]{2,1,0:T(8,128)(2,1)}, u32[]{:S(2)}) copy-start(bf16[1,128,4096]{2,1,0:T(8,128)(2,1)} %param.10) | copy-start | bytes 3145732
  23.5 224.6 %all-to-all-start.1 = ((bf16[128,1,16,4096]{3,2,1,0:T(8,128)(2,1)}), bf16[128,1,16,4096]{3,2,1,0:T(8,128)(2,1)}, u32[]{:S(2)}, u32[]{:S(2)}) async-start(bf16[128,1,16,4096]{3,2,1,0:T(8,128)(2,1)} %bitcast.94), calls=%async_computation.1 | async-start | bytes 33554432 | tf_op jit(solution)/shard_map/all_to_all | solution.py:136
  33.9 9.6 %copy-start.3 = (s32[1,128,8]{1,2,0:T(8,128)S(1)}, s32[1,128,8]{1,2,0:T(8,128)}, u32[]{:S(2)}) copy-start(s32[1,128,8]{1,2,0:T(8,128)} %param.18) | copy-start | bytes 12292
  33.9 9.8 %copy-start.2 = (bf16[4096,128]{1,0:T(8,128)(2,1)S(1)}, bf16[4096,128]{1,0:T(8,128)(2,1)}, u32[]{:S(2)}) copy-start(bf16[4096,128]{1,0:T(8,128)(2,1)} %param.12) | copy-start | bytes 3145732
  248.0 38.4 %all-to-all-start = ((bf16[128,1,16]{2,1,0:T(2,128)(2,1)}), bf16[128,1,16]{2,1,0:T(2,128)(2,1)S(1)}, u32[]{:S(2)}, u32[]{:S(2)}) async-start(bf16[128,1,16]{2,1,0:T(2,128)(2,1)} %reshape.251), calls=%async_computation | async-start | bytes 131072 | tf_op jit(solution)/shard_map/all_to_all | solution.py:143
  286.4 14.9 %all-to-all-start.3 = ((bf16[1,128,16]{2,0,1:T(2,128)(2,1)}), bf16[1,128,16]{2,0,1:T(2,128)(2,1)S(1)}, u32[]{:S(2)}, u32[]{:S(2)}) async-start(bf16[1,128,16]{2,0,1:T(2,128)(2,1)} %convert_element_type.124), calls=%async_computation.3 | async-start | bytes 131072 | tf_op jit(solution)/shard_map/all_to_all | solution.py:168
  320.0 39.2 %all-to-all-start.5 = ((f32[64,32,128]{2,1,0:T(8,128)}), f32[64,32,128]{2,1,0:T(8,128)S(1)}, u32[]{:S(2)}, u32[]{:S(2)}) async-start(f32[64,32,128]{2,1,0:T(8,128)} %reduce_sum.111), calls=%async_computation.5 | async-start | bytes 2097152 | tf_op jit(solution)/shard_map/all_to_all | solution.py:32
  360.5 38.3 %all-to-all-start.6 = ((f32[64,32,128]{2,1,0:T(8,128)}), f32[64,32,128]{2,1,0:T(8,128)S(1)}, u32[]{:S(2)}, u32[]{:S(2)}) async-start(f32[64,32,128]{2,1,0:T(8,128)} %broadcast_in_dim.24), calls=%async_computation.6 | async-start | bytes 2097152 | tf_op jit(solution)/shard_map/all_to_all | solution.py:42
  404.4 232.1 %all-to-all-start.2 = ((bf16[1,128,16,4096]{3,2,0,1:T(8,128)(2,1)}), bf16[1,128,16,4096]{3,2,0,1:T(8,128)(2,1)}, u32[]{:S(2)}, u32[]{:S(2)}) async-start(bf16[1,128,16,4096]{3,2,0,1:T(8,128)(2,1)} %bitcast.95), calls=%async_computation.2 | async-start | bytes 33554432 | tf_op jit(solution)/shard_map/all_to_all | solution.py:161
  636.5 34.8 %copy-start.1 = (bf16[1,128,4096]{2,1,0:T(8,128)(2,1)S(1)}, bf16[1,128,4096]{2,1,0:T(8,128)(2,1)}, u32[]{:S(2)}) copy-start(bf16[1,128,4096]{2,1,0:T(8,128)(2,1)} %param.10) | copy-start | bytes 3145732
where the time goes:
time: 680 us; the launch traced here: 672 us
  waiting for transfers between devices  234 us (34%)
  blocking collectives  189 us (28%)
  matrix products  85.3 us (13%)
  local copies, waits for them, and re-layouts  82.7 us (12%)
  starting transfers between devices  66 us (10%)
  other arithmetic  13 us (2%)
    all_to_all x1, waiting for transfers between devices, shards(): lax.all_to_all(back_rows.reshape(1, devices, capacity, model_width), SEQ_...  220 us
    psum x2, blocking collectives, over_axes(): return functools.reduce(lax.psum, axes, shard)  178 us
    dot_general x1, matrix products, expert_backward(): jnp.einsum('rf,df->rd', grad_first, w_gate, preferred_element_type=jnp.fl...  29.5 us
    dot_general x1, matrix products, expert_backward(): jnp.einsum('rf,df->rd', grad_second, w_up, preferred_element_type=jnp.flo...  27.9 us
    gather x1, local copies, waits for them, and re-layouts, shards(): returned_rows[slot_index].reshape(tok_rows, top_count, model_width)  23.1 us
    dot_general x1, matrix products, expert_backward(): jnp.einsum('rd,fd->rf', grad_rows, w_down, preferred_element_type=jnp.flo...  22.5 us
    all_to_all x1, starting transfers between devices, shards(): lax.all_to_all(gate_slots.reshape(experts, 1, capacity), SEQ_EXP, split_a...  15.1 us
    gather x1, local copies, waits for them, and re-layouts, shards(): grad_slots = grad_padded[slot_token]  14.3 us
  transfers between devices with their start and end apart: 6, of which 3 were waited for; matrix products, arithmetic and copies ran while one was open for 16% of the time, Pallas kernels for 0%

commit v1 on v0

--- a/solution.py
+++ b/solution.py
@@ -8,6 +8,15 @@
 SEQ = ("seq_0", "seq_1")
 EXP = ("exp_0", "exp_1")
 SEQ_EXP = ("seq_0", "seq_1", "exp_0", "exp_1")
+sectors_use = lambda local_values: jnp.concatenate(
+    lax.all_to_all(
+        jnp.stack(jnp.split(local_values, lax.psum(1, axis_name=SEQ_EXP), axis=0)),
+        axis_name=SEQ_EXP,
+        split_axis=0,
+        concat_axis=0,
+    ),
+    axis=1,
+)
 
 
 def over_axes(shard, axes):
@@ -140,13 +149,7 @@
             concat_axis=1,
             tiled=True,
         ),
-        lax.all_to_all(
-            gate_slots.reshape(experts, 1, capacity),
-            SEQ_EXP,
-            split_axis=0,
-            concat_axis=1,
-            tiled=True,
-        ),
+        sectors_use(gate_slots.reshape(experts, 1, capacity)),
     )
     back_rows, slot_combine = expert_backward(
         recv_grad.reshape(-1, model_width),

time: 680 us -> 782 us (1.15)
  local copies, waits for them, and re-layouts: 82.7 us -> 155 us
  blocking collectives: 189 us -> 208 us
  starting transfers between devices: 66 us -> 84.7 us
  waiting for transfers between devices: 234 us -> 225 us
    unnamed x12 -> x139, local copies, waits for them, and re-layouts: 11.1 us -> 83.9 us
    psum x2, blocking collectives: 178 us -> 197 us  [over_axes(): return functools.reduce(lax.psum, axes, shard)]
    all_to_all x1, starting transfers between devices: 9.72 us -> 19.8 us  [summed_rows(): return jnp.sum(lax.all_to_all(own, far, 0, 0, tiled=True), axis=0)]
    all_to_all x1, waiting for transfers between devices: 8.85 us -> 0.01 us  [shards(): lax.all_to_all(grad_slots.reshape(experts, 1, capacity, model_width), SEQ...]
    all_to_all x1, starting transfers between devices: 15.1 us -> 23.7 us  [lax.all_to_all(jnp.stack(jnp.split(local_values, lax.psum(1, axis_name=SE...]
  transfers between devices with their start and end apart: 6 -> 6, of which waited for: 3 -> 2; matrix products, arithmetic and copies ran while one was open for 16% -> 23% of each run, Pallas kernels for 0% -> 0%
where the time goes in v1:
time: 782 us; the launch traced here: 773 us
  waiting for transfers between devices  225 us (29%)
  blocking collectives  208 us (27%)
  local copies, waits for them, and re-layouts  155 us (20%)
  matrix products  85.3 us (11%)
  starting transfers between devices  84.7 us (11%)
  other arithmetic  13 us (2%)
    all_to_all x1, waiting for transfers between devices, shards(): lax.all_to_all(back_rows.reshape(1, devices, capacity, model_width), SEQ_...  220 us
    psum x2, blocking collectives, over_axes(): return functools.reduce(lax.psum, axes, shard)  197 us
    unnamed x139, local copies, waits for them, and re-layouts  83.9 us
    dot_general x1, matrix products, expert_backward(): jnp.einsum('rf,df->rd', grad_first, w_gate, preferred_element_type=jnp.fl...  29.5 us
    dot_general x1, matrix products, expert_backward(): jnp.einsum('rf,df->rd', grad_second, w_up, preferred_element_type=jnp.flo...  27.9 us
    all_to_all x1, starting transfers between devices, lax.all_to_all(jnp.stack(jnp.split(local_values, lax.psum(1, axis_name=SE...  23.7 us
    gather x1, local copies, waits for them, and re-layouts, shards(): returned_rows[slot_index].reshape(tok_rows, top_count, model_width)  23.1 us
    dot_general x1, matrix products, expert_backward(): jnp.einsum('rd,fd->rf', grad_rows, w_down, preferred_element_type=jnp.flo...  22.5 us
  transfers between devices with their start and end apart: 6, of which 2 were waited for; matrix products, arithmetic and copies ran while one was open for 23% of the time, Pallas kernels for 0%

profile of v1, /device:TPU:82, one launch (start us, length us, event | category | flops | bytes accessed | tf_op | source)
XLA Modules:
  0.0 773.0 jit_solution(10596206787214913176)
XLA Ops:
  0.6 0.9 copy.462
  1.7 0.7 broadcast_multiply_fusion
  3.5 4.3 scatter_custom_fusion.1
  7.8 1.3 concatenate.3
  9.2 14.3 %gather_fusion = bf16[2048,4096]{1,0:T(8,128)(2,1)} fusion(bf16[129,4096]{1,0:T(8,128)(2,1)S(1)} %concatenate.3, s32[2048]{0:T(1024)S(1)} %fusion.34), kind=kCustom, calls=%fused_computation | custom fusion | bytes 33562624 | tf_op jit(solution)/shard_map/gather | solution.py:135
  23.5 10.4 %all-to-all-start.1 = ((bf16[128,1,16,4096]{3,2,1,0:T(8,128)(2,1)}), bf16[128,1,16,4096]{3,2,1,0:T(8,128)(2,1)}, u32[]{:S(2)}, u32[]{:S(2)}) async-start(bf16[128,1,16,4096]{3,2,1,0:T(8,128)(2,1)} %bitcast.606), calls=%async_computation.1 | async-start | bytes 33554432 | tf_op jit(solution)/shard_map/all_to_all | solution.py:145
  34.7 7.0 gather_fusion.3
  42.2 134.7 %psum.14 = f32[128]{0:T(128)S(1)} all-reduce(f32[128]{0:T(128)S(1)} %convert_reduce_fusion.3), channel_id=1, replica_groups=mesh['seq_0'=4,'seq_1'=4,'exp_0'=4,'exp_1'=2] {'seq_0'}, use_global_device_ids=true, to_apply=%region_13.14 | all-reduce | flops 128 | bytes 1024 | tf_op jit(solution)/shard_map/psum | solution.py:23
  177.0 62.2 %psum.15 = f32[128]{0:T(128)S(1)} all-reduce(f32[128]{0:T(128)S(1)} %psum.14), channel_id=1, replica_groups=mesh['seq_0'=4,'seq_1'=4,'exp_0'=4,'exp_1'=2] {'seq_1'}, use_global_device_ids=true, to_apply=%region_14.15 | all-reduce | flops 128 | bytes 1024 | tf_op jit(solution)/shard_map/psum | solution.py:23
  240.0 7.6 scatter_custom_fusion
  248.7 0.6 constant_dynamic-update-slice_fusion.125
  249.3 0.6 constant_dynamic-update-slice_fusion.124
  249.9 0.6 constant_dynamic-update-slice_fusion.123
  250.5 0.6 constant_dynamic-update-slice_fusion.122
  251.0 0.6 constant_dynamic-update-slice_fusion.121
  251.6 0.6 constant_dynamic-update-slice_fusion.120
  252.7 0.6 constant_dynamic-update-slice_fusion.118
  255.6 0.6 constant_dynamic-update-slice_fusion.113
  256.2 0.6 constant_dynamic-update-slice_fusion.112
  257.3 0.6 constant_dynamic-update-slice_fusion.110
  257.9 0.6 constant_dynamic-update-slice_fusion.109
  258.5 0.6 constant_dynamic-update-slice_fusion.108
  259.1 0.6 constant_dynamic-update-slice_fusion.107
  259.7 0.6 constant_dynamic-update-slice_fusion.106
  264.3 0.6 constant_dynamic-update-slice_fusion.98
  264.8 0.6 constant_dynamic-update-slice_fusion.97
  265.4 0.6 constant_dynamic-update-slice_fusion.96
  266.5 0.6 constant_dynamic-update-slice_fusion.94
  267.1 0.6 constant_dynamic-update-slice_fusion.93
  267.7 0.6 constant_dynamic-update-slice_fusion.92
  268.3 0.6 constant_dynamic-update-slice_fusion.91
  272.3 0.6 constant_dynamic-update-slice_fusion.84
  272.9 0.6 constant_dynamic-update-slice_fusion.83
  273.4 0.6 constant_dynamic-update-slice_fusion.82
  274.0 0.6 constant_dynamic-update-slice_fusion.81
  274.6 0.6 constant_dynamic-update-slice_fusion.80
  275.7 0.6 constant_dynamic-update-slice_fusion.78
  276.3 0.6 constant_dynamic-update-slice_fusion.77
  279.2 4.7 copy.470
  283.9 4.7 copy.469
  290.9 0.6 constant_dynamic-update-slice_fusion.68
  330.6 23.7 %all-to-all-start = ((bf16[128,1,1,16]{3,2,1,0:T(2,128)(2,1)}), bf16[128,1,1,16]{3,2,1,0:T(2,128)(2,1)S(1)}, u32[]{:S(2)}, u32[]{:S(2)}) async-start(bf16[128,1,1,16]{3,2,1,0:T(2,128)(2,1)} %constant_dynamic-update-slice_fusion), calls=%async_computation | async-start | bytes 131072 | tf_op jit(solution)/shard_map/all_to_all | solution.py:12
  354.4 22.5 %fusion.4 = (bf16[2048]{0:T(1024)(128)(2,1)S(1)}, f32[2048,768]{0,1:T(8,128)}) fusion(bf16[1,2048,768]{1,2,0:T(8,128)(2,1)} %copy.469, bf16[1,2048,768]{1,2,0:T(8,128)(2,1)} %copy.470, bf16[2048,4096]{1,0:T(8,128)(2,1)} %bitcast.139, bf16[1,768,4096]{2,1,0:T(8,128)(2,1)} %param.15), kind=kOutput, calls=%fused_computation.17 | convolution fusion | flops 12899055616 | bytes 35655680 | tf_op jit(solution)/shard_map/rd,fd->rf/dot_general | solution.py:76
  376.9 0.7 convert_element_type.124
  377.6 9.8 %all-to-all-start.3 = ((bf16[1,128,16]{2,0,1:T(2,128)(2,1)}), bf16[1,128,16]{2,0,1:T(2,128)(2,1)S(1)}, u32[]{:S(2)}, u32[]{:S(2)}) async-start(bf16[1,128,16]{2,0,1:T(2,128)(2,1)} %convert_element_type.124), calls=%async_computation.3 | async-start | bytes 131072 | tf_op jit(solution)/shard_map/all_to_all | solution.py:171
  387.7 4.9 all-to-all-done.3
  392.8 6.8 gather_fusion.2
  400.7 1.8 convolution_bitcast_fusion
  402.5 1.9 copy.473
  404.6 5.4 all_to_all.52
  410.0 1.2 reduce_sum.111
  411.2 19.8 %all-to-all-start.5 = ((f32[64,32,128]{2,1,0:T(8,128)}), f32[64,32,128]{2,1,0:T(8,128)S(1)}, u32[]{:S(2)}, u32[]{:S(2)}) async-start(f32[64,32,128]{2,1,0:T(8,128)} %reduce_sum.111), calls=%async_computation.5 | async-start | bytes 2097152 | tf_op jit(solution)/shard_map/all_to_all | solution.py:41
  431.1 29.5 %fusion.10 = f32[2048,4096]{1,0:T(8,128)} fusion(bf16[1,4096,768]{2,1,0:T(8,128)(2,1)} %param.13, f32[2048,768]{0,1:T(8,128)} %get-tuple-element.21, bf16[1,2048,768]{1,2,0:T(8,128)(2,1)} %copy.469, bf16[1,2048,768]{1,2,0:T(8,128)(2,1)} %copy.470, f32[2048]{0:T(1024)S(1)} %reshape.443), kind=kOutput, calls=%fused_computation.23 | convolution fusion | flops 12905349120 | bytes 52436992 | tf_op jit(solution)/shard_map/rf,df->rd/dot_general | solution.py:88
  460.7 1.1 broadcast_in_dim.24
  461.8 10.3 %all-to-all-start.6 = ((f32[64,32,128]{2,1,0:T(8,128)}), f32[64,32,128]{2,1,0:T(8,128)S(1)}, u32[]{:S(2)}, u32[]{:S(2)}) async-start(f32[64,32,128]{2,1,0:T(8,128)} %broadcast_in_dim.24), calls=%async_computation.6 | async-start | bytes 2097152 | tf_op jit(solution)/shard_map/all_to_all | solution.py:51
  472.1 27.9 %add_convert_fusion = bf16[2048,4096]{1,0:T(8,128)(2,1)} fusion(f32[2048,4096]{1,0:T(8,128)} %fusion.10, bf16[1,4096,768]{2,1,0:T(8,128)(2,1)} %param.14, f32[2048,768]{0,1:T(8,128)} %get-tuple-element.21, f32[2048]{0:T(1024)S(1)} %reshape.443, bf16[1,2048,768]{1,2,0:T(8,128)(2,1)} %copy.470), kind=kOutput, calls=%fused_computation.6 | convolution fusion | flops 12914262016 | bytes 66068480 | tf_op jit(solution)/shard_map/rf,df->rd/dot_general | solution.py:89
  500.3 5.4 all_to_all.53
  505.7 10.6 %all-to-all-start.2 = ((bf16[1,128,16,4096]{3,2,0,1:T(8,128)(2,1)}), bf16[1,128,16,4096]{3,2,0,1:T(8,128)(2,1)}, u32[]{:S(2)}, u32[]{:S(2)}) async-start(bf16[1,128,16,4096]{3,2,0,1:T(8,128)(2,1)} %bitcast.607), calls=%async_computation.2 | async-start | bytes 33554432 | tf_op jit(solution)/shard_map/all_to_all | solution.py:164
  516.4 0.7 copy.476
  517.3 0.6 constant_dynamic-slice_fusion
  517.9 219.9 %all-to-all-done.2 = bf16[1,128,16,4096]{3,2,0,1:T(8,128)(2,1)} async-done(((bf16[1,128,16,4096]{3,2,0,1:T(8,128)(2,1)}), bf16[1,128,16,4096]{3,2,0,1:T(8,128)(2,1)}, u32[]{:S(2)}, u32[]{:S(2)}) %all-to-all-start.2) | async-done | bytes 16777248 | tf_op jit(solution)/shard_map/all_to_all | solution.py:164
  737.9 23.1 %gather_fusion.1 = bf16[1024,4096]{1,0:T(8,128)(2,1)} fusion(bf16[2048,4096]{1,0:T(8,128)(2,1)} %bitcast.148, s32[1024]{0:T(1024)S(1)} %broadcast_clamp_fusion), kind=kCustom, calls=%fused_computation.1 | custom fusion | bytes 16781312 | tf_op jit(solution)/shard_map/gather | solution.py:181
  760.9 9.1 %convert_reduce_fusion = f32[128,4096]{1,0:T(8,128)S(1)} fusion(bf16[1024,4096]{1,0:T(8,128)(2,1)} %gather_fusion.1), kind=kLoop, calls=%fused_computation.7 | loop fusion | flops 7864320 | bytes 10485760 | tf_op jit(solution)/shard_map/reduce_sum | solution.py:180
  770.0 2.7 fusion.15
  (157 shorter events, 61.7 us)
Async XLA Ops:
  0.6 33.3 %copy-start = (bf16[1,128,4096]{2,1,0:T(8,128)(2,1)S(1)}, bf16[1,128,4096]{2,1,0:T(8,128)(2,1)}, u32[]{:S(2)}) copy-start(bf16[1,128,4096]{2,1,0:T(8,128)(2,1)} %param.10) | copy-start | bytes 3145732
  23.5 10.4 %copy-start.3 = (s32[1,128,8]{1,2,0:T(8,128)S(1)}, s32[1,128,8]{1,2,0:T(8,128)}, u32[]{:S(2)}) copy-start(s32[1,128,8]{1,2,0:T(8,128)} %param.18) | copy-start | bytes 12292
  23.5 10.4 %copy-start.2 = (bf16[4096,128]{1,0:T(8,128)(2,1)S(1)}, bf16[4096,128]{1,0:T(8,128)(2,1)}, u32[]{:S(2)}) copy-start(bf16[4096,128]{1,0:T(8,128)(2,1)} %param.12) | copy-start | bytes 3145732
  23.5 307.1 %all-to-all-start.1 = ((bf16[128,1,16,4096]{3,2,1,0:T(8,128)(2,1)}), bf16[128,1,16,4096]{3,2,1,0:T(8,128)(2,1)}, u32[]{:S(2)}, u32[]{:S(2)}) async-start(bf16[128,1,16,4096]{3,2,1,0:T(8,128)(2,1)} %bitcast.606), calls=%async_computation.1 | async-start | bytes 33554432 | tf_op jit(solution)/shard_map/all_to_all | solution.py:145
  330.6 47.0 %all-to-all-start = ((bf16[128,1,1,16]{3,2,1,0:T(2,128)(2,1)}), bf16[128,1,1,16]{3,2,1,0:T(2,128)(2,1)S(1)}, u32[]{:S(2)}, u32[]{:S(2)}) async-start(bf16[128,1,1,16]{3,2,1,0:T(2,128)(2,1)} %constant_dynamic-update-slice_fusion), calls=%async_computation | async-start | bytes 131072 | tf_op jit(solution)/shard_map/all_to_all | solution.py:12
  377.6 14.9 %all-to-all-start.3 = ((bf16[1,128,16]{2,0,1:T(2,128)(2,1)}), bf16[1,128,16]{2,0,1:T(2,128)(2,1)S(1)}, u32[]{:S(2)}, u32[]{:S(2)}) async-start(bf16[1,128,16]{2,0,1:T(2,128)(2,1)} %convert_element_type.124), calls=%async_computation.3 | async-start | bytes 131072 | tf_op jit(solution)/shard_map/all_to_all | solution.py:171
  411.2 49.4 %all-to-all-start.5 = ((f32[64,32,128]{2,1,0:T(8,128)}), f32[64,32,128]{2,1,0:T(8,128)S(1)}, u32[]{:S(2)}, u32[]{:S(2)}) async-start(f32[64,32,128]{2,1,0:T(8,128)} %reduce_sum.111), calls=%async_computation.5 | async-start | bytes 2097152 | tf_op jit(solution)/shard_map/all_to_all | solution.py:41
  461.8 38.3 %all-to-all-start.6 = ((f32[64,32,128]{2,1,0:T(8,128)}), f32[64,32,128]{2,1,0:T(8,128)S(1)}, u32[]{:S(2)}, u32[]{:S(2)}) async-start(f32[64,32,128]{2,1,0:T(8,128)} %broadcast_in_dim.24), calls=%async_computation.6 | async-start | bytes 2097152 | tf_op jit(solution)/shard_map/all_to_all | solution.py:51
  505.7 232.1 %all-to-all-start.2 = ((bf16[1,128,16,4096]{3,2,0,1:T(8,128)(2,1)}), bf16[1,128,16,4096]{3,2,0,1:T(8,128)(2,1)}, u32[]{:S(2)}, u32[]{:S(2)}) async-start(bf16[1,128,16,4096]{3,2,0,1:T(8,128)(2,1)} %bitcast.607), calls=%async_computation.2 | async-start | bytes 33554432 | tf_op jit(solution)/shard_map/all_to_all | solution.py:164
  737.9 34.8 %copy-start.1 = (bf16[1,128,4096]{2,1,0:T(8,128)(2,1)S(1)}, bf16[1,128,4096]{2,1,0:T(8,128)(2,1)}, u32[]{:S(2)}) copy-start(bf16[1,128,4096]{2,1,0:T(8,128)(2,1)} %param.10) | copy-start | bytes 3145732
